TPU v7x, 32 devices: a whole 2x2x4 slice. The times are simulated.
32 devices in a mesh: lat: 2 (over y), lon: 4 (over x, core), lev: 4 (over z).
Axes of the slice: x: 2, y: 2, z: 4, core: 2. Of those that a mesh axis runs over, the one named last changes fastest.
Arguments:
- tracer: float32 [8, 512, 128, 128], P('lat', 'lon', 'lev'), may hold values from 0.5 to 2
- conductance: float32 [8, 512, 128, 128], P('lat', 'lon', 'lev'), may hold values from 0.03 to 0.15
- source: float32 [8, 512, 128, 128], P('lat', 'lon', 'lev'), may hold values from -0.2 to 0.2
Outputs:
- standardized: float32 [8, 512, 128, 128], P('lat', 'lon', 'lev')
- tracer_end: float32 [8, 512, 128, 128], P('lat', 'lon', 'lev')
All inputs are finite; a program needn't handle non-finite values.
Results may differ from a plain program's by a relative error of at most 0.00002.
Values sent between devices are 32-bit elements; how exact they have to be, the bound alone decides.
A program may use at most 128 MiB of HBM per device.

v0:
```python
import jax
import jax.numpy as jnp
from jax import lax
from jax.sharding import PartitionSpec as P

STEPS = 3


def padded_2(cells, sides, width):
    for axis, dim in sides:
        count = lax.axis_size(axis)
        ends = count - 1
        head = lax.slice_in_dim(cells, 0, width, axis=dim)
        tail = lax.slice_in_dim(cells, cells.shape[dim] - width, cells.shape[dim], axis=dim)
        cells = jnp.concatenate(
            [
                lax.ppermute(tail, axis, [(i, (i + 1) % count) for i in range(ends)]),
                cells,
                lax.ppermute(head, axis, [((i + 1) % count, i) for i in range(ends)]),
            ],
            axis=dim,
        )
    return cells


def inner_cells(values, dims):
    for dim in dims:
        values = lax.slice_in_dim(values, 1, values.shape[dim] - 1, axis=dim)
    return values


def side_cells(values, dim, start, dims):
    others = [other for other in dims if other != dim]
    values = inner_cells(values, others)
    return lax.slice_in_dim(values, start, start + values.shape[dim] - 2, axis=dim)


def advance(padded, conductance, source):
    middle = inner_cells(padded, (0, 1, 2))
    lower = [side_cells(padded, dim, 0, (0, 1, 2)) for dim in (0, 1, 2)]
    upper = [side_cells(padded, dim, 2, (0, 1, 2)) for dim in (0, 1, 2)]
    spread = lower[0] + upper[0] + lower[1] + upper[1] + lower[2] + upper[2] - 6.0 * middle
    return middle + conductance * spread + source


def shards(tracer, conductance, source):
    for step in range(STEPS):
        padded = padded_2(tracer, (("lat", 0), ("lon", 1), ("lev", 2)), 1)
        tracer = advance(padded, conductance, source)
    count = tracer.shape[1] * lax.axis_size("lon")
    guess = 1.0
    moved = tracer - guess
    totals, squares = lax.psum(
        (jnp.sum(moved, axis=1, keepdims=True), jnp.sum(moved * moved, axis=1, keepdims=True)),
        "lon",
    )
    line_mean = guess + totals / count
    centred = tracer - line_mean
    line_variance = squares / count - totals / count * (totals / count)
    standardized = centred * lax.rsqrt(line_variance + 0.0001)
    return (standardized, tracer)


def solution(mesh):
    placed = (
        P("lat", "lon", "lev", None),
        P("lat", "lon", "lev", None),
        P("lat", "lon", "lev", None),
    )
    return jax.shard_map(
        shards,
        mesh=mesh,
        in_specs=placed,
        out_specs=(P("lat", "lon", "lev", None), P("lat", "lon", "lev", None)),
        check_vma=False,
    )
```

profile of v0, /device:TPU:0, one launch (start us, length us, event | category | flops | bytes accessed | tf_op | source)
XLA Modules:
  0.0 376.3 jit_solution(15974642121828131703)
XLA Ops:
  7.2 4.2 %fusion.31 = (f32[1,128,32,128]{3,2,1,0:T(8,128)}, f32[1,128,32,128]{3,2,1,0:T(8,128)S(1)}) fusion(f32[4,128,32,128]{3,2,1,0:T(8,128)} %param.3), kind=kLoop, calls=%fused_computation.103 | loop fusion | bytes 8388608 | tf_op jit(solution)/shard_map/slice | solution.py:13
  11.4 5.2 %collective-permute-start = (f32[1,128,32,128]{3,2,1,0:T(8,128)S(1)}, f32[1,128,32,128]{3,2,1,0:T(8,128)S(1)}, u32[]{:S(2)}, u32[]{:S(2)}) collective-permute-start(f32[1,128,32,128]{3,2,1,0:T(8,128)S(1)} %get-tuple-element.26), channel_id=1, source_target_pairs={{0,16},{1,17},{2,18},{3,19},{4,20},{5,21},{6,22},{7,23},{8,24},{9,... | collective-permute-start | bytes 6291464 | tf_op jit(solution)/shard_map/ppermute | solution.py:17
  17.8 43.4 %collective-permute-done = f32[1,128,32,128]{3,2,1,0:T(8,128)S(1)} collective-permute-done((f32[1,128,32,128]{3,2,1,0:T(8,128)S(1)}, f32[1,128,32,128]{3,2,1,0:T(8,128)S(1)}, u32[]{:S(2)}, u32[]{:S(2)}) %collective-permute-start) | collective-permute-done | bytes 2097184 | tf_op jit(solution)/shard_map/ppermute | solution.py:17
  63.8 2.1 collective-permute-done.1
  65.8 1.8 constant_dynamic-update-slice_fusion
  69.0 1.6 collective-permute-start.3
  70.5 3.5 collective-permute-done.3
  75.9 4.6 %collective-permute-start.4 = (f32[6,130,1,128]{3,1,2,0:T(8,128)S(1)}, f32[6,130,1,128]{3,1,2,0:T(8,128)S(1)}, u32[]{:S(2)}, u32[]{:S(2)}) collective-permute-start(f32[6,130,1,128]{3,1,2,0:T(8,128)S(1)} %copy.20), channel_id=1, source_target_pairs={{0,1},{1,2},{2,3},{4,5},{5,6},{6,7},{8,9},{9,10},{10,11},{12,13},{... | collective-permute-start | bytes 1198088 | tf_op jit(solution)/shard_map/ppermute | solution.py:17
  80.5 6.2 %collective-permute-done.5 = f32[6,130,1,128]{3,1,2,0:T(8,128)S(1)} collective-permute-done((f32[6,130,1,128]{3,1,2,0:T(8,128)S(1)}, f32[6,130,1,128]{3,1,2,0:T(8,128)S(1)}, u32[]{:S(2)}, u32[]{:S(2)}) %collective-permute-start.5) | collective-permute-done | bytes 399392 | tf_op jit(solution)/shard_map/ppermute | solution.py:19
  87.1 1.4 collective-permute-done.4
  88.9 26.8 %fusion.22 = f32[4,128,32,128]{3,2,1,0:T(8,128)S(1)} fusion(f32[4,128,32,128]{3,2,1,0:T(8,128)} %param.5, f32[4,128,32,128]{3,2,1,0:T(8,128)} %param.3, f32[4,128,32,128]{3,2,1,0:T(8,128)} %param.4, f32[6,130,1,128]{3,2,1,0:T(1,128)S(1)} %copy.23, f32[6,1,32,128]{3,2,1,0:T(8,128)S(1)} %collective-permute-done.3, f32[6,128,32,128]{3,2,1,0:T(8,128)} %copy-done.2, ...), kind=kLoop, calls=%fused_computation.59 | loop fusion | flops 41943040 | bytes 51326976 | tf_op jit(solution)/shard_map/add | solution.py:43
  116.3 2.5 collective-permute-start.6
  120.0 43.4 %collective-permute-done.6 = f32[1,128,32,128]{3,2,1,0:T(8,128)S(1)} collective-permute-done((f32[1,128,32,128]{3,2,1,0:T(8,128)S(1)}, f32[1,128,32,128]{3,2,1,0:T(8,128)S(1)}, u32[]{:S(2)}, u32[]{:S(2)}) %collective-permute-start.6) | collective-permute-done | bytes 2097184 | tf_op jit(solution)/shard_map/ppermute | solution.py:17
  163.5 4.8 %collective-permute-done.7 = f32[1,128,32,128]{3,2,1,0:T(8,128)S(1)} collective-permute-done((f32[1,128,32,128]{3,2,1,0:T(8,128)S(1)}, f32[1,128,32,128]{3,2,1,0:T(8,128)S(1)}, u32[]{:S(2)}, u32[]{:S(2)}) %collective-permute-start.7) | collective-permute-done | bytes 2097184 | tf_op jit(solution)/shard_map/ppermute | solution.py:19
  168.3 2.6 collective-permute-start.8
  172.2 1.9 collective-permute-done.9
  176.6 5.2 %collective-permute-start.10 = (f32[6,130,1,128]{3,1,2,0:T(8,128)S(1)}, f32[6,130,1,128]{3,1,2,0:T(8,128)S(1)}, u32[]{:S(2)}, u32[]{:S(2)}) collective-permute-start(f32[6,130,1,128]{3,1,2,0:T(8,128)S(1)} %copy.24), channel_id=1, source_target_pairs={{0,1},{1,2},{2,3},{4,5},{5,6},{6,7},{8,9},{9,10},{10,11},{12,13},{... | collective-permute-start | bytes 1198088 | tf_op jit(solution)/shard_map/ppermute | solution.py:17
  181.8 6.2 %collective-permute-done.11 = f32[6,130,1,128]{3,1,2,0:T(8,128)S(1)} collective-permute-done((f32[6,130,1,128]{3,1,2,0:T(8,128)S(1)}, f32[6,130,1,128]{3,1,2,0:T(8,128)S(1)}, u32[]{:S(2)}, u32[]{:S(2)}) %collective-permute-start.11) | collective-permute-done | bytes 399392 | tf_op jit(solution)/shard_map/ppermute | solution.py:19
  188.5 1.4 collective-permute-done.10
  190.2 28.8 %fusion.13 = f32[4,128,32,128]{3,2,1,0:T(8,128)} fusion(f32[4,128,32,128]{3,2,1,0:T(8,128)} %param.5, f32[4,128,32,128]{3,2,1,0:T(8,128)} %copy-done.1, f32[4,128,32,128]{3,2,1,0:T(8,128)} %param.4, f32[6,130,1,128]{3,2,1,0:T(1,128)S(1)} %copy.27, f32[6,1,32,128]{3,2,1,0:T(8,128)S(1)} %collective-permute-done.9, ...), kind=kLoop, calls=%fused_computation.32 | loop fusion | flops 58720256 | bytes 38744064 | tf_op jit(solution)/shard_map/add | solution.py:43
  219.1 2.8 fusion.29
  221.9 2.1 collective-permute-start.12
  225.4 43.6 %collective-permute-done.12 = f32[1,128,32,128]{3,2,1,0:T(8,128)S(1)} collective-permute-done((f32[1,128,32,128]{3,2,1,0:T(8,128)S(1)}, f32[1,128,32,128]{3,2,1,0:T(8,128)S(1)}, u32[]{:S(2)}, u32[]{:S(2)}) %collective-permute-start.12) | collective-permute-done | bytes 2097184 | tf_op jit(solution)/shard_map/ppermute | solution.py:17
  269.0 4.8 %collective-permute-done.13 = f32[1,128,32,128]{3,2,1,0:T(8,128)S(1)} collective-permute-done((f32[1,128,32,128]{3,2,1,0:T(8,128)S(1)}, f32[1,128,32,128]{3,2,1,0:T(8,128)S(1)}, u32[]{:S(2)}, u32[]{:S(2)}) %collective-permute-start.13) | collective-permute-done | bytes 2097184 | tf_op jit(solution)/shard_map/ppermute | solution.py:19
  273.8 2.4 collective-permute-start.14
  277.5 1.9 collective-permute-done.15
  281.9 5.3 %collective-permute-start.16 = (f32[6,130,1,128]{3,1,2,0:T(8,128)S(1)}, f32[6,130,1,128]{3,1,2,0:T(8,128)S(1)}, u32[]{:S(2)}, u32[]{:S(2)}) collective-permute-start(f32[6,130,1,128]{3,1,2,0:T(8,128)S(1)} %copy.28), channel_id=1, source_target_pairs={{0,1},{1,2},{2,3},{4,5},{5,6},{6,7},{8,9},{9,10},{10,11},{12,13},{... | collective-permute-start | bytes 1198088 | tf_op jit(solution)/shard_map/ppermute | solution.py:17
  287.2 6.2 %collective-permute-done.17 = f32[6,130,1,128]{3,1,2,0:T(8,128)S(1)} collective-permute-done((f32[6,130,1,128]{3,1,2,0:T(8,128)S(1)}, f32[6,130,1,128]{3,1,2,0:T(8,128)S(1)}, u32[]{:S(2)}, u32[]{:S(2)}) %collective-permute-start.17) | collective-permute-done | bytes 399392 | tf_op jit(solution)/shard_map/ppermute | solution.py:19
  293.8 1.4 collective-permute-done.16
  295.6 29.6 %add_reduce_fusion = (f32[4,32,128]{2,1,0:T(8,128)}, f32[4,32,128]{2,1,0:T(8,128)}, f32[4,128,32,128]{3,2,1,0:T(8,128)}) fusion(f32[4,128,32,128]{3,2,1,0:T(8,128)} %param.5, f32[4,128,32,128]{3,2,1,0:T(8,128)} %fusion.13, f32[4,128,32,128]{3,2,1,0:T(8,128)} %param.4, f32[6,130,1,128]{3,2,1,0:T(1,128)S(1)} %copy.31, ...), kind=kLoop, calls=%fused_computation.75 | loop fusion | flops 67076096 | bytes 38875136 | tf_op jit(solution)/shard_map/reduce_sum | solution.py:54
  325.2 34.9 %all-reduce.3.cloned.1.call-done = (f32[4,1,32,128]{3,2,0,1:T(8,128)}, f32[4,1,32,128]{3,2,0,1:T(8,128)}) async-done(((f32[4,1,32,128]{3,2,0,1:T(8,128)}, f32[4,1,32,128]{3,2,0,1:T(8,128)}), (f32[4,1,32,128]{3,2,0,1:T(8,128)}, f32[4,1,32,128]{3,2,0,1:T(8,128)})) %all-reduce.3.cloned.1.call-update) | async-done | bytes 131088 | tf_op jit(solution)/shard_map/psum | solution.py:53
  361.0 8.5 %subtract_multiply_fusion = f32[4,128,32,128]{3,2,1,0:T(8,128)} fusion(f32[4,128,32,128]{3,2,1,0:T(8,128)} %get-tuple-element.8, f32[4,32,128]{2,1,0:T(8,128)S(1)} %get-tuple-element.28, f32[4,32,128]{2,1,0:T(8,128)S(1)} %get-tuple-element.27), kind=kLoop, calls=%fused_computation.74 | loop fusion | flops 4194304 | bytes 16908288 | tf_op jit(solution)/shard_map/mul | solution.py:60
  (52 shorter events, 21.0 us)
Async XLA Ops:
  7.2 352.9 %all-reduce.3.cloned.1.call-start = ((), (), s32[]{:S(2)}) async-start(), calls=%async_computation | async-start | bytes 262144 | tf_op jit(solution)/shard_map/psum | solution.py:53
  7.2 55.6 %copy-start.3 = (f32[4,128,32,128]{3,2,1,0:T(8,128)S(1)}, f32[4,128,32,128]{3,2,1,0:T(8,128)}, u32[]{:S(2)}) copy-start(f32[4,128,32,128]{3,2,1,0:T(8,128)} %param.3) | copy-start | bytes 25165828
  11.4 49.9 %collective-permute-start = (f32[1,128,32,128]{3,2,1,0:T(8,128)S(1)}, f32[1,128,32,128]{3,2,1,0:T(8,128)S(1)}, u32[]{:S(2)}, u32[]{:S(2)}) collective-permute-start(f32[1,128,32,128]{3,2,1,0:T(8,128)S(1)} %get-tuple-element.26), channel_id=1, source_target_pairs={{0,16},{1,17},{2,18},{3,19},{4,20},{5,21},{6,22},{7,23},{8,24},{9,... | collective-permute-start | bytes 6291464 | tf_op jit(solution)/shard_map/ppermute | solution.py:17
  16.5 49.3 %collective-permute-start.1 = (f32[1,128,32,128]{3,2,1,0:T(8,128)}, f32[1,128,32,128]{3,2,1,0:T(8,128)}, u32[]{:S(2)}, u32[]{:S(2)}) collective-permute-start(f32[1,128,32,128]{3,2,1,0:T(8,128)} %get-tuple-element.25), channel_id=1, source_target_pairs={{16,0},{17,1},{18,2},{19,3},{20,4},{21,5},{22,6},{23,7},{24,8},{25... | collective-permute-start | bytes 6291464 | tf_op jit(solution)/shard_map/ppermute | solution.py:19
  61.3 1.3 copy-start.6
  67.6 20.9 %copy-start.2 = (f32[6,128,32,128]{3,2,1,0:T(8,128)}, f32[6,128,32,128]{3,2,1,0:T(8,128)S(1)}, u32[]{:S(2)}) copy-start(f32[6,128,32,128]{3,2,1,0:T(8,128)S(1)} %constant_dynamic-update-slice_fusion) | copy-start | bytes 37748740
  67.6 2.9 collective-permute-start.2
  68.9 20.0 %copy-start.7 = (f32[1,128,32,128]{3,2,1,0:T(8,128)S(1)}, f32[1,128,32,128]{3,2,1,0:T(8,128)}, u32[]{:S(2)}) copy-start(f32[1,128,32,128]{3,2,1,0:T(8,128)} %copy-done.6) | copy-start | bytes 6291460
  69.0 5.0 %collective-permute-start.3 = (f32[6,1,32,128]{3,2,1,0:T(8,128)S(1)}, f32[6,1,32,128]{3,2,1,0:T(8,128)S(1)}, u32[]{:S(2)}, u32[]{:S(2)}) collective-permute-start(f32[6,1,32,128]{3,2,1,0:T(8,128)S(1)} %get-tuple-element.20), channel_id=1, source_target_pairs={{4,0},{8,4},{12,8},{5,1},{9,5},{13,9},{6,2},{10,6},{14,10},{7,3},{... | collective-permute-start | bytes 294920 | tf_op jit(solution)/shard_map/ppermute | solution.py:19
  74.6 12.1 %collective-permute-start.5 = (f32[6,130,1,128]{3,1,2,0:T(8,128)S(1)}, f32[6,130,1,128]{3,1,2,0:T(8,128)S(1)}, u32[]{:S(2)}, u32[]{:S(2)}) collective-permute-start(f32[6,130,1,128]{3,1,2,0:T(8,128)S(1)} %copy.22), channel_id=1, source_target_pairs={{1,0},{2,1},{3,2},{5,4},{6,5},{7,6},{9,8},{10,9},{11,10},{13,12},{... | collective-permute-start | bytes 1198088 | tf_op jit(solution)/shard_map/ppermute | solution.py:19
  75.9 12.6 %collective-permute-start.4 = (f32[6,130,1,128]{3,1,2,0:T(8,128)S(1)}, f32[6,130,1,128]{3,1,2,0:T(8,128)S(1)}, u32[]{:S(2)}, u32[]{:S(2)}) collective-permute-start(f32[6,130,1,128]{3,1,2,0:T(8,128)S(1)} %copy.20), channel_id=1, source_target_pairs={{0,1},{1,2},{2,3},{4,5},{5,6},{6,7},{8,9},{9,10},{10,11},{12,13},{... | collective-permute-start | bytes 1198088 | tf_op jit(solution)/shard_map/ppermute | solution.py:17
  115.8 58.3 %copy-start.1 = (f32[4,128,32,128]{3,2,1,0:T(8,128)}, f32[4,128,32,128]{3,2,1,0:T(8,128)S(1)}, u32[]{:S(2)}) copy-start(f32[4,128,32,128]{3,2,1,0:T(8,128)S(1)} %fusion.22) | copy-start | bytes 25165828
  116.3 47.2 %collective-permute-start.6 = (f32[1,128,32,128]{3,2,1,0:T(8,128)S(1)}, f32[1,128,32,128]{3,2,1,0:T(8,128)S(1)}, u32[]{:S(2)}, u32[]{:S(2)}) collective-permute-start(f32[1,128,32,128]{3,2,1,0:T(8,128)S(1)} %get-tuple-element.23), channel_id=1, source_target_pairs={{0,16},{1,17},{2,18},{3,19},{4,20},{5,21},{6,22},{7,23},{8,24},{9,... | collective-permute-start | bytes 6291464 | tf_op jit(solution)/shard_map/ppermute | solution.py:17
  118.7 49.5 %collective-permute-start.7 = (f32[1,128,32,128]{3,2,1,0:T(8,128)S(1)}, f32[1,128,32,128]{3,2,1,0:T(8,128)S(1)}, u32[]{:S(2)}, u32[]{:S(2)}) collective-permute-start(f32[1,128,32,128]{3,2,1,0:T(8,128)S(1)} %get-tuple-element.24), channel_id=1, source_target_pairs={{16,0},{17,1},{18,2},{19,3},{20,4},{21,5},{22,6},{23,7},{24,8},{25... | collective-permute-start | bytes 6291464 | tf_op jit(solution)/shard_map/ppermute | solution.py:19
  168.3 6.9 %copy-start.5 = (f32[1,128,32,128]{3,2,1,0:T(8,128)}, f32[1,128,32,128]{3,2,1,0:T(8,128)S(1)}, u32[]{:S(2)}) copy-start(f32[1,128,32,128]{3,2,1,0:T(8,128)S(1)} %collective-permute-done.7) | copy-start | bytes 6291460
  168.3 3.9 %collective-permute-start.8 = (f32[6,1,32,128]{3,2,1,0:T(8,128)S(1)}, f32[6,1,32,128]{3,2,1,0:T(8,128)S(1)}, u32[]{:S(2)}, u32[]{:S(2)}) collective-permute-start(f32[6,1,32,128]{3,2,1,0:T(8,128)S(1)} %get-tuple-element.17), channel_id=1, source_target_pairs={{0,4},{4,8},{8,12},{1,5},{5,9},{9,13},{2,6},{6,10},{10,14},{3,7},{... | collective-permute-start | bytes 294920 | tf_op jit(solution)/shard_map/ppermute | solution.py:17
  170.9 3.2 collective-permute-start.9
  175.2 12.8 %collective-permute-start.11 = (f32[6,130,1,128]{3,1,2,0:T(8,128)S(1)}, f32[6,130,1,128]{3,1,2,0:T(8,128)S(1)}, u32[]{:S(2)}, u32[]{:S(2)}) collective-permute-start(f32[6,130,1,128]{3,1,2,0:T(8,128)S(1)} %copy.26), channel_id=1, source_target_pairs={{1,0},{2,1},{3,2},{5,4},{6,5},{7,6},{9,8},{10,9},{11,10},{13,12},{... | collective-permute-start | bytes 1198088 | tf_op jit(solution)/shard_map/ppermute | solution.py:19
  176.6 13.3 %collective-permute-start.10 = (f32[6,130,1,128]{3,1,2,0:T(8,128)S(1)}, f32[6,130,1,128]{3,1,2,0:T(8,128)S(1)}, u32[]{:S(2)}, u32[]{:S(2)}) collective-permute-start(f32[6,130,1,128]{3,1,2,0:T(8,128)S(1)} %copy.24), channel_id=1, source_target_pairs={{0,1},{1,2},{2,3},{4,5},{5,6},{6,7},{8,9},{9,10},{10,11},{12,13},{... | collective-permute-start | bytes 1198088 | tf_op jit(solution)/shard_map/ppermute | solution.py:17
  219.1 54.7 %copy-start = (f32[4,128,32,128]{3,2,1,0:T(8,128)S(1)}, f32[4,128,32,128]{3,2,1,0:T(8,128)}, u32[]{:S(2)}) copy-start(f32[4,128,32,128]{3,2,1,0:T(8,128)} %fusion.13) | copy-start | bytes 25165828
  221.9 47.1 %collective-permute-start.12 = (f32[1,128,32,128]{3,2,1,0:T(8,128)S(1)}, f32[1,128,32,128]{3,2,1,0:T(8,128)S(1)}, u32[]{:S(2)}, u32[]{:S(2)}) collective-permute-start(f32[1,128,32,128]{3,2,1,0:T(8,128)S(1)} %get-tuple-element.21), channel_id=1, source_target_pairs={{0,16},{1,17},{2,18},{3,19},{4,20},{5,21},{6,22},{7,23},{8,24},{9,... | collective-permute-start | bytes 6291464 | tf_op jit(solution)/shard_map/ppermute | solution.py:17
  224.1 49.7 %collective-permute-start.13 = (f32[1,128,32,128]{3,2,1,0:T(8,128)S(1)}, f32[1,128,32,128]{3,2,1,0:T(8,128)S(1)}, u32[]{:S(2)}, u32[]{:S(2)}) collective-permute-start(f32[1,128,32,128]{3,2,1,0:T(8,128)S(1)} %get-tuple-element.22), channel_id=1, source_target_pairs={{16,0},{17,1},{18,2},{19,3},{20,4},{21,5},{22,6},{23,7},{24,8},{25... | collective-permute-start | bytes 6291464 | tf_op jit(solution)/shard_map/ppermute | solution.py:19
  273.8 6.7 %copy-start.4 = (f32[1,128,32,128]{3,2,1,0:T(8,128)}, f32[1,128,32,128]{3,2,1,0:T(8,128)S(1)}, u32[]{:S(2)}) copy-start(f32[1,128,32,128]{3,2,1,0:T(8,128)S(1)} %collective-permute-done.13) | copy-start | bytes 6291460
  273.8 3.7 collective-permute-start.14
  276.2 3.2 collective-permute-start.15
  280.6 12.8 %collective-permute-start.17 = (f32[6,130,1,128]{3,1,2,0:T(8,128)S(1)}, f32[6,130,1,128]{3,1,2,0:T(8,128)S(1)}, u32[]{:S(2)}, u32[]{:S(2)}) collective-permute-start(f32[6,130,1,128]{3,1,2,0:T(8,128)S(1)} %copy.30), channel_id=1, source_target_pairs={{1,0},{2,1},{3,2},{5,4},{6,5},{7,6},{9,8},{10,9},{11,10},{13,12},{... | collective-permute-start | bytes 1198088 | tf_op jit(solution)/shard_map/ppermute | solution.py:19
  281.9 13.3 %collective-permute-start.16 = (f32[6,130,1,128]{3,1,2,0:T(8,128)S(1)}, f32[6,130,1,128]{3,1,2,0:T(8,128)S(1)}, u32[]{:S(2)}, u32[]{:S(2)}) collective-permute-start(f32[6,130,1,128]{3,1,2,0:T(8,128)S(1)} %copy.28), channel_id=1, source_target_pairs={{0,1},{1,2},{2,3},{4,5},{5,6},{6,7},{8,9},{9,10},{10,11},{12,13},{... | collective-permute-start | bytes 1198088 | tf_op jit(solution)/shard_map/ppermute | solution.py:17
Sparse Core Ops, SparseCore 0:
  325.3 34.7 all-reduce.2
where the time goes:
time: 377 us; the launch traced here: 376 us
  waiting for transfers between devices  207 us (55%)
  other arithmetic  97.4 us (26%)
  starting transfers between devices  43 us (11%)
  local copies, waits for them, and re-layouts  14.4 us (4%)
  between operations  14.4 us (4%)
    ppermute x9, waiting for transfers between devices, padded_2(): lax.ppermute(tail, axis, [(i, (i + 1) % count) for i in range(ends)])  135 us
    add x2, other arithmetic, advance(): return middle + conductance * spread + source  55.7 us
    ppermute x9, waiting for transfers between devices, padded_2(): lax.ppermute(head, axis, [((i + 1) % count, i) for i in range(ends)])  37.6 us
    psum x1, waiting for transfers between devices, shards(): lax.psum((jnp.sum(moved, axis=1, keepdims=True), jnp.sum(moved * moved, a...  34.9 us
    ppermute x9, starting transfers between devices, padded_2(): lax.ppermute(tail, axis, [(i, (i + 1) % count) for i in range(ends)])  31.1 us
    reduce_sum x1, other arithmetic, shards(): jnp.sum(moved, axis=1, keepdims=True)  29.6 us
    ppermute x9, starting transfers between devices, padded_2(): lax.ppermute(head, axis, [((i + 1) % count, i) for i in range(ends)])  11.9 us
    mul x1, other arithmetic, shards(): standardized = centred * lax.rsqrt(line_variance + 0.0001)  8.48 us
  transfers between devices with their start and end apart: 19, of which 16 were waited for; matrix products, arithmetic and copies ran while one was open for 1% of the time, Pallas kernels for 0%

commit v1 on v0

v1 whole, which is shorter than its diff:
```python
import functools

import jax
import jax.numpy as jnp
from jax import lax
from jax.experimental import pallas as pl
from jax.experimental.pallas import tpu as pltpu
from jax.sharding import PartitionSpec as P

STEPS = 3
GUESS = 1.0
TILE = 8
ROWS = 8


def kernel(
    sizes, tracer, conductance, source, end, mean_out, scale_out,
    even, odd, cond, sour, z_lower, z_upper, z_first, z_last, sums, peer_sums,
    load_sem, y_send, y_recv, x_send, x_recv, z_send, z_recv, sum_send, sum_recv,
):
    n_lat, n_lon, n_lev = sizes
    J, I, K, M = tracer.shape
    chunks = K // TILE
    blocks = I // ROWS
    count = I * n_lon
    lat, lon, lev = lax.axis_index("lat"), lax.axis_index("lon"), lax.axis_index("lev")
    below = {"lat": lat > 0, "lon": lon > 0, "lev": lev > 0}
    above = {"lat": lat < n_lat - 1, "lon": lon < n_lon - 1, "lev": lev < n_lev - 1}
    index = {"lat": lat, "lon": lon, "lev": lev}
    field = [even, odd]

    def levels(chunk):
        return pl.ds(chunk * TILE, TILE)

    def target(axis, way):
        return {axis: index[axis] + (1 if way == 0 else -1)}

    def y_copy(step, chunk, way):
        plane = J - 1 if way == 0 else 0
        if step == 0:
            src = tracer.at[plane, :, levels(chunk), :]
        else:
            src = field[step % 2].at[plane + 1, pl.ds(1, I), levels(chunk), :]
        dst = field[step % 2].at[0 if way == 0 else J + 1, pl.ds(1, I), levels(chunk), :]
        return pltpu.make_async_remote_copy(
            src_ref=src, dst_ref=dst, send_sem=y_send.at[step, chunk, way],
            recv_sem=y_recv.at[step, chunk, way], device_id=target("lat", way),
            device_id_type=pl.DeviceIdType.MESH)

    def x_copy(step, way):
        buf = field[step % 2]
        return pltpu.make_async_remote_copy(
            src_ref=buf.at[pl.ds(1, J), I if way == 0 else 1],
            dst_ref=buf.at[pl.ds(1, J), 0 if way == 0 else I + 1],
            send_sem=x_send.at[step, way], recv_sem=x_recv.at[step, way],
            device_id=target("lon", way), device_id_type=pl.DeviceIdType.MESH)

    def z_copy(step, way):
        src = z_last if way == 0 else z_first
        dst = z_lower if way == 0 else z_upper
        return pltpu.make_async_remote_copy(
            src_ref=src.at[step % 2], dst_ref=dst.at[step % 2],
            send_sem=z_send.at[step, way], recv_sem=z_recv.at[step, way],
            device_id=target("lev", way), device_id_type=pl.DeviceIdType.MESH)

    def sum_copy(chunk, shift):
        return pltpu.make_async_remote_copy(
            src_ref=sums.at[chunk], dst_ref=peer_sums.at[shift - 1, chunk],
            send_sem=sum_send.at[chunk, shift - 1], recv_sem=sum_recv.at[chunk, shift - 1],
            device_id={"lon": lax.rem(lon + shift, n_lon)}, device_id_type=pl.DeviceIdType.MESH)

    def sends(axis, way, act):
        pl.when((above if way == 0 else below)[axis])(act)

    def arrives(axis, way, act):
        pl.when((below if way == 0 else above)[axis])(act)

    barrier = pltpu.get_barrier_semaphore()
    met = n_lon - 1
    for axis in ("lat", "lev"):
        for way in (0, 1):
            def greet(axis=axis, way=way):
                pl.semaphore_signal(barrier, inc=1, device_id=target(axis, way),
                                    device_id_type=pl.DeviceIdType.MESH)
            sends(axis, way, greet)
        met = met + below[axis].astype(jnp.int32) + above[axis].astype(jnp.int32)
    for shift in range(1, n_lon):
        pl.semaphore_signal(barrier, inc=1, device_id={"lon": lax.rem(lon + shift, n_lon)},
                            device_id_type=pl.DeviceIdType.MESH)

    loads = [
        pltpu.make_async_copy(tracer, even.at[pl.ds(1, J), pl.ds(1, I)], load_sem.at[0]),
        pltpu.make_async_copy(conductance, cond, load_sem.at[1]),
        pltpu.make_async_copy(source, sour, load_sem.at[2]),
    ]
    loads[0].start()
    pl.semaphore_wait(barrier, met)

    for chunk in range(chunks):
        for way in (0, 1):
            sends("lat", way, lambda: y_copy(0, chunk, way).start())
    loads[1].start()
    loads[2].start()

    for way in (0, 1):
        def no_y():
            @pl.loop(0, blocks)
            def _(b):
                for buf in field:
                    buf[0 if way == 0 else J + 1, pl.ds(1 + b * ROWS, ROWS)] = jnp.zeros(
                        (ROWS, K, M), jnp.float32)
        pl.when(jnp.logical_not((below if way == 0 else above)["lat"]))(no_y)

        def no_x():
            for buf in field:
                for j in range(J):
                    buf[1 + j, 0 if way == 0 else I + 1] = jnp.zeros((K, M), jnp.float32)
        pl.when(jnp.logical_not((below if way == 0 else above)["lon"]))(no_x)

        def no_z():
            @pl.loop(0, blocks)
            def _(b):
                for p in range(2):
                    for j in range(J):
                        (z_lower if way == 0 else z_upper)[p, j, pl.ds(b * ROWS, ROWS)] = (
                            jnp.zeros((ROWS, 1, M), jnp.float32))
        pl.when(jnp.logical_not((below if way == 0 else above)["lev"]))(no_z)

    def pack_and_send(step):
        buf = field[step % 2]
        for way in (0, 1):
            sends("lon", way, lambda: x_copy(step, way).start())

        @pl.loop(0, J * blocks)
        def _(q):
            j, r = q // blocks, (q % blocks) * ROWS
            z_first[step % 2, j, pl.ds(r, ROWS)] = buf[1 + j, pl.ds(1 + r, ROWS), pl.ds(0, 1), :]
            z_last[step % 2, j, pl.ds(r, ROWS)] = buf[1 + j, pl.ds(1 + r, ROWS), pl.ds(K - 1, 1), :]

        for way in (0, 1):
            sends("lev", way, lambda: z_copy(step, way).start())

    def next_rows(step, chunk, j, r):
        buf = field[step % 2]
        here = levels(chunk)
        mid = buf[1 + j, pl.ds(1 + r, ROWS), here, :]
        k = lax.broadcasted_iota(jnp.int32, mid.shape, 1)
        if chunk == 0:
            edge = jnp.broadcast_to(z_lower[step % 2, j, pl.ds(r, ROWS)], mid.shape)
        else:
            edge = pltpu.roll(buf[1 + j, pl.ds(1 + r, ROWS), levels(chunk - 1), :], 1, 1)
        k_lower = jnp.where(k == 0, edge, pltpu.roll(mid, 1, 1))
        if chunk == chunks - 1:
            edge = jnp.broadcast_to(z_upper[step % 2, j, pl.ds(r, ROWS)], mid.shape)
        else:
            edge = pltpu.roll(buf[1 + j, pl.ds(1 + r, ROWS), levels(chunk + 1), :], TILE - 1, 1)
        k_upper = jnp.where(k == TILE - 1, edge, pltpu.roll(mid, TILE - 1, 1))
        spread = (
            buf[j, pl.ds(1 + r, ROWS), here, :] + buf[2 + j, pl.ds(1 + r, ROWS), here, :]
            + buf[1 + j, pl.ds(r, ROWS), here, :] + buf[1 + j, pl.ds(2 + r, ROWS), here, :]
            + k_lower + k_upper - 6.0 * mid)
        return mid + cond[j, pl.ds(r, ROWS), here, :] * spread + sour[j, pl.ds(r, ROWS), here, :]

    def planes(step, chunk, first, number):
        if step < STEPS - 1:
            to = field[(step + 1) % 2]

            @pl.loop(0, number * blocks)
            def _(q):
                j, r = first + q // blocks, (q % blocks) * ROWS
                to[1 + j, pl.ds(1 + r, ROWS), levels(chunk), :] = next_rows(step, chunk, j, r)
        else:
            @pl.loop(0, number)
            def _(p):
                j = first + p

                def body(b, totals):
                    new = next_rows(step, chunk, j, b * ROWS)
                    end[j, pl.ds(b * ROWS, ROWS), levels(chunk), :] = new
                    moved = new - GUESS
                    return (totals[0] + jnp.sum(moved, axis=0),
                            totals[1] + jnp.sum(moved * moved, axis=0))

                zero = jnp.zeros((TILE, M), jnp.float32)
                total, square = lax.fori_loop(0, blocks, body, (zero, zero))
                sums[chunk, 0, j] = total
                sums[chunk, 1, j] = square

    def y_arrives(step, chunk, way):
        arrives("lat", way, lambda: y_copy(step, chunk, way).wait_recv())

    early = jnp.where(lat == 0, 0, J - 1)
    late = J - 1 - early

    loads[0].wait()
    pack_and_send(0)
    loads[1].wait()
    loads[2].wait()
    for step in range(STEPS):
        if step >= 1:
            for way in (0, 1):
                sends("lon", way, lambda: x_copy(step - 1, way).wait_send())
                sends("lev", way, lambda: z_copy(step - 1, way).wait_send())
                for chunk in range(chunks):
                    sends("lat", way, lambda: y_copy(step - 1, chunk, way).wait_send())
        for way in (0, 1):
            arrives("lon", way, lambda: x_copy(step, way).wait_recv())
            arrives("lev", way, lambda: z_copy(step, way).wait_recv())
        if step == STEPS - 1:
            for chunk in range(chunks):
                planes(step, chunk, 1, J - 2)
        for chunk in range(chunks):
            if step < STEPS - 1:
                planes(step, chunk, 1, J - 2)
            pl.when(jnp.logical_and(lat > 0, lat < n_lat - 1))(
                lambda: y_copy(step, chunk, 1).wait_recv())
            planes(step, chunk, early, 1)
            pl.when(lat > 0)(lambda: y_copy(step, chunk, 0).wait_recv())
            pl.when(jnp.logical_and(lat == 0, lat < n_lat - 1))(
                lambda: y_copy(step, chunk, 1).wait_recv())
            planes(step, chunk, late, 1)
            if step < STEPS - 1:
                for way in (0, 1):
                    sends("lat", way, lambda: y_copy(step + 1, chunk, way).start())
            else:
                for shift in range(1, n_lon):
                    sum_copy(chunk, shift).start()
        if step < STEPS - 1:
            pack_and_send(step + 1)

    for chunk in range(chunks):
        for shift in range(1, n_lon):
            sum_copy(chunk, shift).wait_recv()
        total = sums[chunk]
        for shift in range(1, n_lon):
            total = total + peer_sums[shift - 1, chunk]
        offset = total[0] / count
        variance = total[1] / count - offset * offset
        mean_out[:, levels(chunk), :] = GUESS + offset
        scale_out[:, levels(chunk), :] = lax.rsqrt(variance + 0.0001)

    for chunk in range(chunks):
        for shift in range(1, n_lon):
            sum_copy(chunk, shift).wait_send()
        for way in (0, 1):
            sends("lat", way, lambda: y_copy(STEPS - 1, chunk, way).wait_send())
    for way in (0, 1):
        sends("lon", way, lambda: x_copy(STEPS - 1, way).wait_send())
        sends("lev", way, lambda: z_copy(STEPS - 1, way).wait_send())


def shards(sizes, tracer, conductance, source):
    n_lat, n_lon, n_lev = sizes
    J, I, K, M = tracer.shape
    chunks = K // TILE
    f32 = jnp.float32
    dma = pltpu.SemaphoreType.DMA
    peers = max(n_lon - 1, 1)
    end, mean, scale = pl.pallas_call(
        functools.partial(kernel, sizes),
        out_shape=[
            pltpu.VMEM((J, I, K, M), f32),
            jax.ShapeDtypeStruct((J, K, M), f32),
            jax.ShapeDtypeStruct((J, K, M), f32),
        ],
        in_specs=[pl.BlockSpec(memory_space=pltpu.HBM)] * 3,
        out_specs=[pl.BlockSpec(memory_space=pltpu.VMEM)] * 3,
        scratch_shapes=[
            pltpu.VMEM((J + 2, I + 2, K, M), f32),
            pltpu.VMEM((J + 2, I + 2, K, M), f32),
            pltpu.VMEM((J, I, K, M), f32),
            pltpu.VMEM((J, I, K, M), f32),
            pltpu.VMEM((2, J, I, 1, M), f32),
            pltpu.VMEM((2, J, I, 1, M), f32),
            pltpu.VMEM((2, J, I, 1, M), f32),
            pltpu.VMEM((2, J, I, 1, M), f32),
            pltpu.VMEM((chunks, 2, J, TILE, M), f32),
            pltpu.VMEM((peers, chunks, 2, J, TILE, M), f32),
            dma((3,)),
            dma((STEPS, chunks, 2)),
            dma((STEPS, chunks, 2)),
            dma((STEPS, 2)),
            dma((STEPS, 2)),
            dma((STEPS, 2)),
            dma((STEPS, 2)),
            dma((chunks, peers)),
            dma((chunks, peers)),
        ],
        compiler_params=pltpu.CompilerParams(
            collective_id=0, has_side_effects=True, vmem_limit_bytes=47 * 1024 * 1024),
    )(tracer, conductance, source)
    standardized = (end - mean[:, None]) * scale[:, None]
    return (standardized, end)


def solution(mesh):
    placed = P("lat", "lon", "lev", None)
    sizes = tuple(mesh.shape[axis] for axis in ("lat", "lon", "lev"))
    return jax.shard_map(
        functools.partial(shards, sizes),
        mesh=mesh,
        in_specs=(placed, placed, placed),
        out_specs=(placed, placed),
        check_vma=False,
    )
```

time: 377 us -> 156 us (0.41)
  waiting for transfers between devices: 207 us -> 0 us
  Pallas kernels: 0 us -> 146 us
  other arithmetic: 97.4 us -> 5.94 us
  starting transfers between devices: 43 us -> 0 us
  between operations: 14.4 us -> 0.64 us
  local copies, waits for them, and re-layouts: 14.4 us -> 3.4 us
    ppermute x18 -> x0, waiting for transfers between devices: 172 us -> none  [the longest x9 135 us: padded_2(): lax.ppermute(tail, axis, [(i, (i + 1) % count) for i in range(ends)])]
    pallas_call x0 -> x1, Pallas kernels: none -> 146 us  [shards(): pl.pallas_call(functools.partial(kernel, sizes), out_shape=[pltpu.VMEM((J...]
    add x2 -> x0, other arithmetic: 55.7 us -> none  [advance(): return middle + conductance * spread + source]
    ppermute x18 -> x0, starting transfers between devices: 43 us -> none  [the longest x9 31.1 us: padded_2(): lax.ppermute(tail, axis, [(i, (i + 1) % count) for i in range(ends)])]
    psum x1 -> x0, waiting for transfers between devices: 34.9 us -> none  [shards(): lax.psum((jnp.sum(moved, axis=1, keepdims=True), jnp.sum(moved * moved, a...]
    reduce_sum x1 -> x0, other arithmetic: 29.6 us -> none  [shards(): jnp.sum(moved, axis=1, keepdims=True)]
    slice x10 -> x0, local copies, waits for them, and re-layouts: 7.63 us -> none  [the longest x4 4.24 us: padded_2(): head = lax.slice_in_dim(cells, 0, width, axis=dim)]
  transfers between devices with their start and end apart: 19 -> 0, of which waited for: 16 -> 0; matrix products, arithmetic and copies ran while one was open for 1% -> 0% of each run, Pallas kernels for 0% -> 0%
where the time goes in v1:
time: 156 us
  Pallas kernels  146 us (94%)
  other arithmetic  5.94 us (4%)
  local copies, waits for them, and re-layouts  3.4 us (2%)
    pallas_call x1, Pallas kernels, shards(): pl.pallas_call(functools.partial(kernel, sizes), out_shape=[pltpu.VMEM((J...  146 us
    mul x1, other arithmetic, shards(): standardized = (end - mean[:, None]) * scale[:, None]  5.94 us
    unnamed x1, local copies, waits for them, and re-layouts  3.4 us

profile of v1, /device:TPU:0, one launch (start us, length us, event | category | flops | bytes accessed | tf_op | source)
XLA Modules:
  0.0 155.6 jit_solution(8594372727197775899)
XLA Ops:
  0.6 145.6 %shard_map.50 = (f32[4,128,32,128]{3,2,1,0:T(8,128)S(1)}, f32[4,32,128]{2,1,0:T(8,128)}, f32[4,32,128]{2,1,0:T(8,128)}) custom-call(f32[4,128,32,128]{3,2,1,0:T(8,128)} %tracer.1, f32[4,128,32,128]{3,2,1,0:T(8,128)} %conductance.1, f32[4,128,32,128]{3,2,1,0:T(8,128)} %source.1), custom_call_target="tpu_custom_call" | custom-call | tf_op jit(solution)/shard_map/pallas_call | solution.py:259
  146.2 5.9 %subtract_multiply_fusion = f32[4,128,32,128]{3,2,1,0:T(8,128)} fusion(f32[4,128,32,128]{3,2,1,0:T(8,128)S(1)} %get-tuple-element.9, f32[4,32,128]{2,1,0:T(8,128)} %get-tuple-element.7, f32[4,32,128]{2,1,0:T(8,128)} %get-tuple-element.6), kind=kLoop, calls=%fused_computation | loop fusion | flops 4194304 | bytes 16908288 | tf_op jit(solution)/shard_map/mul | solution.py:292
  152.2 3.4 %copy.6 = f32[4,128,32,128]{3,2,1,0:T(8,128)} copy(f32[4,128,32,128]{3,2,1,0:T(8,128)S(1)} %get-tuple-element.9) | data formatting | bytes 16777216

commit v2 on v1

--- a/solution.py
+++ b/solution.py
@@ -63,10 +63,16 @@
             send_sem=z_send.at[step, way], recv_sem=z_recv.at[step, way],
             device_id=target("lev", way), device_id_type=pl.DeviceIdType.MESH)
 
-    def sum_copy(chunk, shift):
+    early = jnp.where(lat == 0, 0, J - 1)
+    late = J - 1 - early
+    parts = [pl.ds(jnp.where(lat == 0, 0, 1), J - 1), pl.ds(late, 1)]
+
+    def sum_copy(chunk, shift, part):
         return pltpu.make_async_remote_copy(
-            src_ref=sums.at[chunk], dst_ref=peer_sums.at[shift - 1, chunk],
-            send_sem=sum_send.at[chunk, shift - 1], recv_sem=sum_recv.at[chunk, shift - 1],
+            src_ref=sums.at[chunk, parts[part]],
+            dst_ref=peer_sums.at[shift - 1, chunk, parts[part]],
+            send_sem=sum_send.at[chunk, shift - 1, part],
+            recv_sem=sum_recv.at[chunk, shift - 1, part],
             device_id={"lon": lax.rem(lon + shift, n_lon)}, device_id_type=pl.DeviceIdType.MESH)
 
     def sends(axis, way, act):
@@ -183,14 +189,11 @@
 
                 zero = jnp.zeros((TILE, M), jnp.float32)
                 total, square = lax.fori_loop(0, blocks, body, (zero, zero))
-                sums[chunk, 0, j] = total
-                sums[chunk, 1, j] = square
+                sums[chunk, j, 0] = total
+                sums[chunk, j, 1] = square
 
     def y_arrives(step, chunk, way):
         arrives("lat", way, lambda: y_copy(step, chunk, way).wait_recv())
-
-    early = jnp.where(lat == 0, 0, J - 1)
-    late = J - 1 - early
 
     loads[0].wait()
     pack_and_send(0)
@@ -215,6 +218,9 @@
             pl.when(jnp.logical_and(lat > 0, lat < n_lat - 1))(
                 lambda: y_copy(step, chunk, 1).wait_recv())
             planes(step, chunk, early, 1)
+            if step == STEPS - 1:
+                for shift in range(1, n_lon):
+                    sum_copy(chunk, shift, 0).start()
             pl.when(lat > 0)(lambda: y_copy(step, chunk, 0).wait_recv())
             pl.when(jnp.logical_and(lat == 0, lat < n_lat - 1))(
                 lambda: y_copy(step, chunk, 1).wait_recv())
@@ -224,29 +230,50 @@
                     sends("lat", way, lambda: y_copy(step + 1, chunk, way).start())
             else:
                 for shift in range(1, n_lon):
-                    sum_copy(chunk, shift).start()
+                    sum_copy(chunk, shift, 1).start()
         if step < STEPS - 1:
             pack_and_send(step + 1)
 
     for chunk in range(chunks):
         for shift in range(1, n_lon):
-            sum_copy(chunk, shift).wait_recv()
+            for part in (0, 1):
+                sum_copy(chunk, shift, part).wait_recv()
         total = sums[chunk]
         for shift in range(1, n_lon):
             total = total + peer_sums[shift - 1, chunk]
-        offset = total[0] / count
-        variance = total[1] / count - offset * offset
+        offset = total[:, 0] / count
+        variance = total[:, 1] / count - offset * offset
         mean_out[:, levels(chunk), :] = GUESS + offset
         scale_out[:, levels(chunk), :] = lax.rsqrt(variance + 0.0001)
 
     for chunk in range(chunks):
         for shift in range(1, n_lon):
-            sum_copy(chunk, shift).wait_send()
+            for part in (0, 1):
+                sum_copy(chunk, shift, part).wait_send()
         for way in (0, 1):
             sends("lat", way, lambda: y_copy(STEPS - 1, chunk, way).wait_send())
     for way in (0, 1):
         sends("lon", way, lambda: x_copy(STEPS - 1, way).wait_send())
         sends("lev", way, lambda: z_copy(STEPS - 1, way).wait_send())
+
+
+def write_out(end, mean, scale, standardized, end_out, held, sem):
+    J, I, K, M = end.shape
+    keep = pltpu.make_async_copy(end, end_out, sem.at[J])
+    keep.start()
+    copies = []
+    for j in range(J):
+        offset, factor = mean[j], scale[j]
+
+        @pl.loop(0, I // ROWS)
+        def _(b):
+            rows = pl.ds(b * ROWS, ROWS)
+            held[j, rows] = (end[j, rows] - offset) * factor
+
+        copies.append(pltpu.make_async_copy(held.at[j], standardized.at[j], sem.at[j]))
+        copies[-1].start()
+    for copy in copies + [keep]:
+        copy.wait()
 
 
 def shards(sizes, tracer, conductance, source):
@@ -260,8 +287,8 @@
         functools.partial(kernel, sizes),
         out_shape=[
             pltpu.VMEM((J, I, K, M), f32),
-            jax.ShapeDtypeStruct((J, K, M), f32),
-            jax.ShapeDtypeStruct((J, K, M), f32),
+            pltpu.VMEM((J, K, M), f32),
+            pltpu.VMEM((J, K, M), f32),
         ],
         in_specs=[pl.BlockSpec(memory_space=pltpu.HBM)] * 3,
         out_specs=[pl.BlockSpec(memory_space=pltpu.VMEM)] * 3,
@@ -274,8 +301,8 @@
             pltpu.VMEM((2, J, I, 1, M), f32),
             pltpu.VMEM((2, J, I, 1, M), f32),
             pltpu.VMEM((2, J, I, 1, M), f32),
-            pltpu.VMEM((chunks, 2, J, TILE, M), f32),
-            pltpu.VMEM((peers, chunks, 2, J, TILE, M), f32),
+            pltpu.VMEM((chunks, J, 2, TILE, M), f32),
+            pltpu.VMEM((peers, chunks, J, 2, TILE, M), f32),
             dma((3,)),
             dma((STEPS, chunks, 2)),
             dma((STEPS, chunks, 2)),
@@ -283,14 +310,20 @@
             dma((STEPS, 2)),
             dma((STEPS, 2)),
             dma((STEPS, 2)),
-            dma((chunks, peers)),
-            dma((chunks, peers)),
+            dma((chunks, peers, 2)),
+            dma((chunks, peers, 2)),
         ],
         compiler_params=pltpu.CompilerParams(
             collective_id=0, has_side_effects=True, vmem_limit_bytes=47 * 1024 * 1024),
     )(tracer, conductance, source)
-    standardized = (end - mean[:, None]) * scale[:, None]
-    return (standardized, end)
+    return pl.pallas_call(
+        write_out,
+        out_shape=[jax.ShapeDtypeStruct((J, I, K, M), f32)] * 2,
+        in_specs=[pl.BlockSpec(memory_space=pltpu.VMEM)] * 3,
+        out_specs=[pl.BlockSpec(memory_space=pltpu.HBM)] * 2,
+        scratch_shapes=[pltpu.VMEM((J, I, K, M), f32), dma((J + 1,))],
+        compiler_params=pltpu.CompilerParams(vmem_limit_bytes=32 * 1024 * 1024),
+    )(end, mean, scale)
 
 
 def solution(mesh):

time: 156 us -> 152 us (0.974)
  other arithmetic: 5.94 us -> 0 us
  Pallas kernels: 146 us -> 151 us
  local copies, waits for them, and re-layouts: 3.4 us -> 0 us
    pallas_call x0 -> x1, Pallas kernels: none -> 6.02 us  [shards(): pl.pallas_call(write_out, out_shape=[jax.ShapeDtypeStruct((J, I, K, M), f...]
    mul x1 -> x0, other arithmetic: 5.94 us -> none  [shards(): standardized = (end - mean[:, None]) * scale[:, None]]
    unnamed x1 -> x0, local copies, waits for them, and re-layouts: 3.4 us -> none
where the time goes in v2:
time: 152 us
  Pallas kernels  151 us (99%)
    pallas_call x1, Pallas kernels, shards(): pl.pallas_call(functools.partial(kernel, sizes), out_shape=[pltpu.VMEM((J...  145 us
    pallas_call x1, Pallas kernels, shards(): pl.pallas_call(write_out, out_shape=[jax.ShapeDtypeStruct((J, I, K, M), f...  6.02 us

profile of v2, /device:TPU:0, one launch (start us, length us, event | category | flops | bytes accessed | tf_op | source)
XLA Modules:
  0.0 151.6 jit_solution(3916055887855932038)
XLA Ops:
  0.6 144.9 %shard_map.50 = (f32[4,128,32,128]{3,2,1,0:T(8,128)S(1)}, f32[4,32,128]{2,1,0:T(8,128)S(1)}, f32[4,32,128]{2,1,0:T(8,128)S(1)}) custom-call(f32[4,128,32,128]{3,2,1,0:T(8,128)} %tracer.1, f32[4,128,32,128]{3,2,1,0:T(8,128)} %conductance.1, f32[4,128,32,128]{3,2,1,0:T(8,128)} %source.1), custom_call_target="tpu_custom_call" | custom-call | tf_op jit(solution)/shard_map/pallas_call | solution.py:286
  145.6 6.0 %shard_map.51 = (f32[4,128,32,128]{3,2,1,0:T(8,128)}, f32[4,128,32,128]{3,2,1,0:T(8,128)}) custom-call(f32[4,128,32,128]{3,2,1,0:T(8,128)S(1)} %get-tuple-element.5.end, f32[4,32,128]{2,1,0:T(8,128)S(1)} %get-tuple-element.6.mean, f32[4,32,128]{2,1,0:T(8,128)S(1)} %get-tuple-element.7.scale), custom_call_target="tpu_custom_call" | custom-call | tf_op jit(solution)/shard_map/pallas_call | solution.py:319
